TPU v7x, 32 devices: a whole 2x2x4 slice. The times are simulated.
32 devices in a mesh: section: 2 (over x), expert: 4 (over y, core), dp: 4 (over z).
Axes of the slice: x: 2, y: 2, z: 4, core: 2. Of those that a mesh axis runs over, the one named last changes fastest.
Arguments:
- x_in: bfloat16 [8, 256, 2048], P(None, ('expert', 'dp'), 'section'), may hold values from -6 to 6
- cotangent: bfloat16 [8, 256, 2048], P(None, ('expert', 'dp'), 'section'), may hold values from -6 to 6
- route_ids: int32 [2, 8, 256, 2], P('section', None, ('expert', 'dp')), may hold values from 0 to 15, all different within a row; in each aligned block of 16 rows (0 to 15, 16 to 31, ..., all dimensions but the last counted through in order) at most 2 rows name the same one
- norm_gain: float32 [2, 2048], P('section'), may hold values from 0.5 to 1.5
- router: bfloat16 [2, 2048, 16], P('section'), may hold values from -0.125 to 0.125
- w_gate_up: bfloat16 [2, 16, 2048, 1024], P('section', ('expert', 'dp')), may hold values from -0.125 to 0.125
- w_down: bfloat16 [2, 16, 512, 2048], P('section', ('expert', 'dp')), may hold values from -0.25 to 0.25
Outputs:
- grad_in: bfloat16 [8, 256, 2048], P(None, ('expert', 'dp'), 'section')
- grad_gate_up: float32 [2, 16, 2048, 1024], P('section', ('expert', 'dp'))
- grad_down: float32 [2, 16, 512, 2048], P('section', ('expert', 'dp'))
- grad_router: float32 [2, 2048, 16], P('section')
- grad_gain: float32 [2, 2048], P('section')
Inputs may be any that keep to these rules, and one draw needn't show every extreme that they name: `route_ids`: each row names two different experts; the 16 rows of one device in one layer and micro-batch name any expert at most 2 times, a bound that some block reaches in some of them.
All inputs are finite; a program needn't handle non-finite values.
Results may differ from a plain program's by a relative error of at most 0.035.
Values may be sent and summed in bfloat16 or wider, within the bound.
A program may use at most 64 MiB of HBM per device.

v0:
```python
import jax
import jax.numpy as jnp
from jax import lax
from jax.sharding import PartitionSpec as P

EPS = 1e-05


def shifted(value, axis, steps):
    count = lax.axis_size(axis)
    leading, last = (max(0, -steps), min(count, count - steps))
    return lax.ppermute(value, axis, [(source, source + steps) for source in range(leading, last)])


def keep_row(stash, position, value, active):
    old_row = lax.dynamic_index_in_dim(stash, position, 0, keepdims=False)
    return lax.dynamic_update_index_in_dim(stash, jnp.where(active, value, old_row), position, 0)


def slot_tables(route_rows, n_expert, capacity):
    experts = jnp.arange(n_expert, dtype=jnp.int32)
    expert_hits = (route_rows[:, :, None] == experts).astype(jnp.int32)
    per_expert = jnp.sum(expert_hits, axis=1)
    before = jnp.cumsum(per_expert, axis=0) - per_expert
    slot_ids = jnp.sum(expert_hits * before[:, None, :], axis=2)
    dest_cell = jnp.transpose(route_rows * capacity + slot_ids)
    cell_ids = jnp.arange(n_expert * capacity, dtype=jnp.int32)
    slot_place = (dest_cell[:, :, None] == cell_ids).astype(jnp.bfloat16)
    return (expert_hits.astype(jnp.float32), slot_place)


def norm_rows(layer_in, gain_vec):
    h_wide = layer_in.astype(jnp.float32)
    inv_rms = lax.rsqrt(jnp.mean(h_wide * h_wide, axis=-1, keepdims=True) + EPS)
    normed = (h_wide * inv_rms * gain_vec).astype(jnp.bfloat16)
    return (h_wide, inv_rms, normed)


def pair_gates(normed, router_mat, expert_hits):
    logits = jnp.dot(normed, router_mat, preferred_element_type=jnp.float32)
    chosen = jnp.sum(expert_hits * logits[:, None, :], axis=2)
    return (
        jax.nn.sigmoid(chosen[:, 0] - chosen[:, 1]),
        jax.nn.sigmoid(chosen[:, 1] - chosen[:, 0]),
    )


def expert_inner(exp_rows, w_gu):
    gate_up = jnp.einsum("sekd,edf->sekf", exp_rows, w_gu, preferred_element_type=jnp.float32)
    half_cols = w_gu.shape[2] // 2
    gate_part = gate_up[..., :half_cols]
    up_part = gate_up[..., half_cols:]
    sigmoid_gate = jax.nn.sigmoid(gate_part)
    hidden = (gate_part * sigmoid_gate * up_part).astype(jnp.bfloat16)
    return (gate_part, up_part, sigmoid_gate, hidden)


def expert_grads(gate_part, up_part, sigmoid_gate, dy_rows, w_gu, w_dn):
    d_hidden = jnp.einsum("sekd,efd->sekf", dy_rows, w_dn, preferred_element_type=jnp.float32)
    silu_gate = gate_part * sigmoid_gate
    silu_slope = sigmoid_gate * (1.0 + gate_part * (1.0 - sigmoid_gate))
    gate_up_grad = jnp.concatenate(
        [d_hidden * up_part * silu_slope, d_hidden * silu_gate], axis=-1
    ).astype(jnp.bfloat16)
    rows_grad = jnp.einsum(
        "sekf,edf->sekd", gate_up_grad, w_gu, preferred_element_type=jnp.float32
    ).astype(jnp.bfloat16)
    return (gate_up_grad, rows_grad)


def local(x_in, cotangent, route_ids, norm_gain, router, w_gate_up, w_down):
    micro_count, tok_rows, _ = x_in.shape
    n_segment = lax.axis_size("section")
    n_rank = lax.axis_size("expert") * lax.axis_size("dp")
    per_rank = w_down.shape[1]
    hidden_width = w_down.shape[2]
    model_width = w_down.shape[3]
    n_expert = per_rank * n_rank
    capacity = tok_rows * 2 * 9 // (8 * n_expert)
    cells = n_expert * capacity
    segment_idx = lax.axis_index("section")
    rows_shape = (n_rank, per_rank, capacity, model_width)
    x_all, top_all = (
        lax.all_gather(x_in, "section", axis=2, tiled=True),
        lax.all_gather(cotangent, "section", axis=2, tiled=True),
    )
    route_all = route_ids[0]
    gain_vec = norm_gain[0]
    router_mat = router[0]
    router_wide = router_mat.astype(jnp.float32)
    w_gu = w_gate_up[0]
    w_dn = w_down[0]
    ticks = micro_count + n_segment - 1

    def expert_forward(piece_rows):
        _, _, _, hidden = expert_inner(piece_rows, w_gu)
        out_rows = jnp.einsum(
            "sekf,efd->sekd", hidden, w_dn, preferred_element_type=jnp.float32
        ).astype(jnp.bfloat16)
        return (
            lax.all_to_all(out_rows, ("expert", "dp"), split_axis=0, concat_axis=0, tiled=True),
            piece_rows,
        )

    def forward_tick(tick_no, state_in):
        received, stash_h, stash_y, stash_x = state_in
        tick_slot = tick_no - segment_idx
        active = (tick_slot >= 0) & (tick_slot < micro_count)
        micro_idx = jnp.clip(tick_slot, 0, micro_count - 1)
        fresh_in = lax.dynamic_index_in_dim(x_all, micro_idx, 0, keepdims=False)
        layer_in = jnp.where(segment_idx == 0, fresh_in, received)
        h_wide, inv_rms, normed = norm_rows(layer_in, gain_vec)
        route_rows = lax.dynamic_index_in_dim(route_all, micro_idx, 0, keepdims=False)
        expert_hits, slot_place = slot_tables(route_rows, n_expert, capacity)
        send_rows = jnp.einsum("ktc,td->cd", slot_place, normed, preferred_element_type=jnp.float32)
        send_rows = send_rows.astype(jnp.bfloat16).reshape(rows_shape)
        returned, landed = expert_forward(
            lax.all_to_all(send_rows, ("expert", "dp"), split_axis=0, concat_axis=0, tiled=True)
        )
        back_flat = returned.reshape(cells, model_width)
        picked = jnp.einsum(
            "ktc,cd->ktd", slot_place, back_flat, preferred_element_type=jnp.float32
        )
        first_gate, second_gate = pair_gates(normed, router_mat, expert_hits)
        layer_out = (
            h_wide + first_gate[:, None] * picked[0] + second_gate[:, None] * picked[1]
        ).astype(jnp.bfloat16)
        passed = shifted(layer_out, "section", 1)
        stash_h = keep_row(stash_h, micro_idx, layer_in, active)
        stash_y = keep_row(stash_y, micro_idx, back_flat, active)
        stash_x = keep_row(stash_x, micro_idx, landed, active)
        return (passed, stash_h, stash_y, stash_x)

    start_fwd = (
        jnp.zeros((tok_rows, model_width), jnp.bfloat16),
        jnp.zeros((micro_count, tok_rows, model_width), jnp.bfloat16),
        jnp.zeros((micro_count, cells, model_width), jnp.bfloat16),
        jnp.zeros((micro_count,) + rows_shape, jnp.bfloat16),
    )
    _, stash_h, stash_y, stash_x = lax.fori_loop(0, ticks, forward_tick, start_fwd)

    def backward_tick(tick_no, state_in):
        received, keep_rows, keep_dy, keep_hidden, keep_dab, stash_grad, acc_router, acc_gain = (
            state_in
        )
        tick_slot = tick_no - (n_segment - 1 - segment_idx)
        active = (tick_slot >= 0) & (tick_slot < micro_count)
        micro_idx = jnp.clip(tick_slot, 0, micro_count - 1)
        fresh_top = lax.dynamic_index_in_dim(top_all, micro_idx, 0, keepdims=False)
        grad_top = jnp.where(segment_idx == n_segment - 1, fresh_top, received)
        grad_wide = grad_top.astype(jnp.float32)
        layer_in = lax.dynamic_index_in_dim(stash_h, micro_idx, 0, keepdims=False)
        h_wide, inv_rms, normed = norm_rows(layer_in, gain_vec)
        route_rows = lax.dynamic_index_in_dim(route_all, micro_idx, 0, keepdims=False)
        expert_hits, slot_place = slot_tables(route_rows, n_expert, capacity)
        first_gate, second_gate = pair_gates(normed, router_mat, expert_hits)
        gates = jnp.stack([first_gate, second_gate])
        scaled = (gates[:, :, None] * grad_wide[None]).astype(jnp.bfloat16)
        dy_send = jnp.einsum("ktc,ktd->cd", slot_place, scaled, preferred_element_type=jnp.float32)
        dy_send = dy_send.astype(jnp.bfloat16).reshape(rows_shape)
        exp_rows = lax.dynamic_index_in_dim(stash_x, micro_idx, 0, keepdims=False)
        dy_rows = lax.all_to_all(dy_send, ("expert", "dp"), split_axis=0, concat_axis=0, tiled=True)
        gate_part, up_part, sigmoid_gate, hidden = expert_inner(exp_rows, w_gu)
        gate_up_grad, rows_grad = expert_grads(
            gate_part, up_part, sigmoid_gate, dy_rows, w_gu, w_dn
        )
        back_grad = lax.all_to_all(
            rows_grad, ("expert", "dp"), split_axis=0, concat_axis=0, tiled=True
        )
        back_y = lax.dynamic_index_in_dim(stash_y, micro_idx, 0, keepdims=False)
        keep_dy = keep_row(keep_dy, micro_idx, dy_rows, active)
        keep_hidden = keep_row(keep_hidden, micro_idx, hidden, active)
        keep_dab = keep_row(keep_dab, micro_idx, gate_up_grad, active)
        normed_grad = jnp.einsum(
            "ktc,cd->td",
            slot_place,
            back_grad.reshape(cells, model_width),
            preferred_element_type=jnp.float32,
        )
        picked = jnp.einsum("ktc,cd->ktd", slot_place, back_y, preferred_element_type=jnp.float32)
        gate_grad = jnp.sum(grad_wide[None] * picked, axis=-1)
        logit_grad = first_gate * second_gate * (gate_grad[0] - gate_grad[1])
        logit_cols = logit_grad[:, None] * (expert_hits[:, 0, :] - expert_hits[:, 1, :])
        normed_grad = normed_grad + jnp.dot(
            logit_cols, router_wide.T, precision=lax.Precision.HIGHEST
        )
        router_term = jnp.dot(
            normed.astype(jnp.float32).T, logit_cols, precision=lax.Precision.HIGHEST
        )
        acc_router = acc_router + jnp.where(active, router_term, 0.0)
        acc_gain = acc_gain + jnp.where(
            active, jnp.sum(normed_grad * h_wide * inv_rms, axis=0), 0.0
        )
        scaled_grad = normed_grad * gain_vec
        projection = jnp.mean(scaled_grad * h_wide, axis=-1, keepdims=True)
        input_grad = (
            grad_wide + inv_rms * scaled_grad - h_wide * inv_rms * inv_rms * inv_rms * projection
        )
        grad_sent = input_grad.astype(jnp.bfloat16)
        stash_grad = keep_row(stash_grad, micro_idx, grad_sent, active)
        passed = shifted(grad_sent, "section", -1)
        return (passed, keep_rows, keep_dy, keep_hidden, keep_dab, stash_grad, acc_router, acc_gain)

    start_bwd = (
        jnp.zeros((tok_rows, model_width), jnp.bfloat16),
        stash_x,
        jnp.zeros((micro_count,) + rows_shape, jnp.bfloat16),
        jnp.zeros((micro_count, n_rank, per_rank, capacity, hidden_width), jnp.bfloat16),
        jnp.zeros((micro_count, n_rank, per_rank, capacity, 2 * hidden_width), jnp.bfloat16),
        jnp.zeros((micro_count, tok_rows, model_width), jnp.bfloat16),
        jnp.zeros((model_width, n_expert), jnp.float32),
        jnp.zeros((model_width,), jnp.float32),
    )
    final = lax.fori_loop(0, ticks, backward_tick, start_bwd)
    _, keep_rows, keep_dy, keep_hidden, keep_dab, stash_grad, acc_router, acc_gain = final
    grad_gu = jnp.einsum(
        "msekd,msekf->edf", keep_rows, keep_dab, preferred_element_type=jnp.float32
    )
    grad_dn = jnp.einsum(
        "msekf,msekd->efd", keep_hidden, keep_dy, preferred_element_type=jnp.float32
    )
    sum_router, sum_gain = (
        lax.psum(acc_router.astype(jnp.bfloat16), ("expert", "dp")).astype(jnp.float32),
        lax.psum(acc_gain.astype(jnp.bfloat16), ("expert", "dp")).astype(jnp.float32),
    )
    first_term = jnp.where(segment_idx == 0, stash_grad.astype(jnp.float32), 0.0)
    grad_in = lax.psum_scatter(
        first_term.astype(jnp.bfloat16), "section", scatter_dimension=2, tiled=True
    )
    return (grad_in, grad_gu[None], grad_dn[None], sum_router[None], sum_gain[None])


def solution(mesh):
    in_specs = (
        P(None, ("expert", "dp"), "section"),
        P(None, ("expert", "dp"), "section"),
        P("section", None, ("expert", "dp"), None),
        P("section", None),
        P("section", None, None),
        P("section", ("expert", "dp"), None, None),
        P("section", ("expert", "dp"), None, None),
    )
    out_specs = (
        P(None, ("expert", "dp"), "section"),
        P("section", ("expert", "dp"), None, None),
        P("section", ("expert", "dp"), None, None),
        P("section", None, None),
        P("section", None),
    )
    return jax.shard_map(local, mesh=mesh, in_specs=in_specs, out_specs=out_specs, check_vma=False)
```

profile of v0, /device:TPU:8, one launch (start us, length us, event | category | flops | bytes accessed | tf_op | source)
XLA Modules:
  0.0 864.4 jit_solution(11679668147466827216)
XLA Ops:
  8.1 10.6 %all_gather.6 = bf16[8,16,2048]{2,1,0:T(8,128)(2,1)} all-gather(bf16[8,16,1024]{2,1,0:T(8,128)(2,1)} %param.12), channel_id=1, replica_groups=mesh['section'=2,'expert'=4,'dp'=4] {'section'}, dimensions={2}, use_global_device_ids=true | all-gather | bytes 786432 | tf_op jit(solution)/shard_map/all_gather | solution.py:85
  18.6 8.9 %all_gather.7 = bf16[8,16,2048]{2,1,0:T(8,128)(2,1)} all-gather(bf16[8,16,1024]{2,1,0:T(8,128)(2,1)} %param.11), channel_id=1, replica_groups=mesh['section'=2,'expert'=4,'dp'=4] {'section'}, dimensions={2}, use_global_device_ids=true | all-gather | bytes 786432 | tf_op jit(solution)/shard_map/all_gather | solution.py:84
  31.9 327.4 %while.48 = (s32[]{:T(128)}, bf16[16,2048]{1,0:T(8,128)(2,1)S(1)}, bf16[8,16,2048]{2,1,0:T(8,128)(2,1)S(1)}, bf16[8,32,2048]{2,1,0:T(8,128)(2,1)}, bf16[8,16,1,2...) while((s32[]{:T(128)}, bf16[16,2048]{1,0:T(8,128)(2,1)S(1)}, ...), condition=%wide.region_7.8_spmd, body=%wide.region_0.7_spmd.sunk | while | flops 209598352 | bytes 11630114 | solution.py:140
  35.7 6.3 all-to-all-start
  52.2 4.8 all-to-all-start.1
  57.8 5.3 all-to-all-done.1
  72.5 4.8 all-to-all-start
  79.6 3.8 all-to-all-done
  87.7 4.8 all-to-all-start.1
  93.3 5.3 all-to-all-done.1
  98.9 4.3 collective-permute-start
  108.9 4.8 all-to-all-start
  115.9 3.8 all-to-all-done
  124.0 4.8 all-to-all-start.1
  129.6 5.3 all-to-all-done.1
  135.2 4.3 collective-permute-start
  145.2 4.8 all-to-all-start
  152.2 3.8 all-to-all-done
  160.3 4.8 all-to-all-start.1
  165.9 5.3 all-to-all-done.1
  171.6 4.3 collective-permute-start
  181.5 4.8 all-to-all-start
  196.6 4.8 all-to-all-start.1
  202.2 5.3 all-to-all-done.1
  207.9 4.3 collective-permute-start
  217.8 4.8 all-to-all-start
  233.0 4.8 all-to-all-start.1
  238.5 5.3 all-to-all-done.1
  244.2 4.3 collective-permute-start
  254.1 4.8 all-to-all-start
  269.3 4.8 all-to-all-start.1
  274.9 5.3 all-to-all-done.1
  280.5 4.3 collective-permute-start
  290.5 4.8 all-to-all-start
  305.6 4.8 all-to-all-start.1
  311.2 5.3 all-to-all-done.1
  316.8 4.3 collective-permute-start
  326.8 4.8 all-to-all-start
  341.9 4.8 all-to-all-start.1
  347.5 5.3 all-to-all-done.1
  353.2 4.3 collective-permute-start
  363.5 403.9 %while.49 = (s32[]{:T(128)}, bf16[16,2048]{1,0:T(8,128)(2,1)S(1)}, bf16[8,16,1,2,2048]{4,3,1,2,0:T(2,128)(2,1)}, bf16[8,16,1,2,512]{4,1,3,2,0:T(8,128)(2,1)}, bf...) while((s32[]{:T(128)}, bf16[16,2048]{1,0:T(8,128)(2,1)S(1)}, ...), condition=%wide.region_18.19_spmd.clone, body=%wide.region_8.18_spmd.clone.sunk | while | flops 361911744 | bytes 17806364 | solution.py:214
  369.7 4.8 all-to-all-start.2
  387.4 6.1 all-to-all-start.3
  404.1 4.2 collective-permute-done.1
  414.5 4.8 all-to-all-start.2
  432.2 6.1 all-to-all-start.3
  459.4 4.8 all-to-all-start.2
  477.1 6.1 all-to-all-start.3
  504.3 4.8 all-to-all-start.2
  522.0 6.1 all-to-all-start.3
  549.2 4.8 all-to-all-start.2
  566.9 6.1 all-to-all-start.3
  594.0 4.8 all-to-all-start.2
  611.7 6.1 all-to-all-start.3
  638.9 4.8 all-to-all-start.2
  656.6 6.1 all-to-all-start.3
  683.8 4.8 all-to-all-start.2
  701.5 6.1 all-to-all-start.3
  728.7 4.8 all-to-all-start.2
  746.4 6.1 all-to-all-start.3
  770.1 6.2 convolution_bitcast_fusion.1
  776.3 32.1 %psum.15 = bf16[1,2048]{1,0:T(2,128)(2,1)S(1)} all-reduce(bf16[1,2048]{1,0:T(2,128)(2,1)S(1)} %broadcast_in_dim.182), channel_id=1, replica_groups=mesh['section'=2,'expert'=4,'dp'=4] {'expert','dp'}, use_global_device_ids=true, to_apply=%region_21.22 | all-reduce | flops 2048 | bytes 8192 | tf_op jit(solution)/shard_map/psum | solution.py:224
  812.1 43.3 %all-reduce.2.cloned.1.call-done = bf16[1,2048,16]{1,2,0:T(8,128)(2,1)} async-done(((bf16[1,2048,16]{1,2,0:T(8,128)(2,1)}), bf16[1,2048,16]{1,2,0:T(8,128)(2,1)}) %all-reduce.2.cloned.1.call-update) | async-done | bytes 65552 | tf_op jit(solution)/shard_map/psum | solution.py:223
  (697 shorter events, 462.8 us)
Async XLA Ops:
  8.0 23.9 %copy-start.2 = (f32[1,2048]{1,0:T(1,128)S(1)}, f32[1,2048]{1,0:T(1,128)}, u32[]{:S(2)}) copy-start(f32[1,2048]{1,0:T(1,128)} %param.14) | copy-start | bytes 24580
  8.0 23.9 %copy-start = (bf16[1,1,512,2048]{3,2,1,0:T(8,128)(2,1)S(1)}, bf16[1,1,512,2048]{3,2,1,0:T(8,128)(2,1)}, u32[]{:S(2)}) copy-start(bf16[1,1,512,2048]{3,2,1,0:T(8,128)(2,1)} %param.17) | copy-start | bytes 6291460
  8.0 847.5 %all-reduce.2.cloned.1.call-start = ((), (), s32[]{:S(2)}) async-start(), calls=%async_computation.6 | async-start | bytes 131072 | tf_op jit(solution)/shard_map/psum | solution.py:223
  35.7 12.3 %all-to-all-start = ((bf16[16,1,2,2048]{3,2,1,0:T(2,128)(2,1)}), bf16[16,1,2,2048]{3,2,1,0:T(2,128)(2,1)S(1)}, u32[]{:S(2)}, u32[]{:S(2)}) async-start(bf16[16,1,2,2048]{3,2,1,0:T(2,128)(2,1)} %bitcast.324), calls=%async_computation | async-start | bytes 262144 | tf_op jit(solution)/shard_map/while/body/eval_jaxpr/all_to_all | solution.py:118
  52.2 10.9 %all-to-all-start.1 = ((bf16[16,1,2,2048]{3,2,1,0:T(2,128)(2,1)}), bf16[16,1,2,2048]{3,2,1,0:T(2,128)(2,1)S(1)}, u32[]{:S(2)}, u32[]{:S(2)}) async-start(bf16[16,1,2,2048]{3,2,1,0:T(2,128)(2,1)} %copy.84), calls=%async_computation.1 | async-start | bytes 262144 | tf_op jit(solution)/shard_map/while/body/eval_jaxpr/all_to_all | solution.py:101
  63.5 5.3 collective-permute-start
  72.5 10.9 %all-to-all-start = ((bf16[16,1,2,2048]{3,2,1,0:T(2,128)(2,1)}), bf16[16,1,2,2048]{3,2,1,0:T(2,128)(2,1)S(1)}, u32[]{:S(2)}, u32[]{:S(2)}) async-start(bf16[16,1,2,2048]{3,2,1,0:T(2,128)(2,1)} %bitcast.324), calls=%async_computation | async-start | bytes 262144 | tf_op jit(solution)/shard_map/while/body/eval_jaxpr/all_to_all | solution.py:118
  87.7 10.9 %all-to-all-start.1 = ((bf16[16,1,2,2048]{3,2,1,0:T(2,128)(2,1)}), bf16[16,1,2,2048]{3,2,1,0:T(2,128)(2,1)S(1)}, u32[]{:S(2)}, u32[]{:S(2)}) async-start(bf16[16,1,2,2048]{3,2,1,0:T(2,128)(2,1)} %copy.84), calls=%async_computation.1 | async-start | bytes 262144 | tf_op jit(solution)/shard_map/while/body/eval_jaxpr/all_to_all | solution.py:101
  98.9 6.2 collective-permute-start
  108.9 10.9 %all-to-all-start = ((bf16[16,1,2,2048]{3,2,1,0:T(2,128)(2,1)}), bf16[16,1,2,2048]{3,2,1,0:T(2,128)(2,1)S(1)}, u32[]{:S(2)}, u32[]{:S(2)}) async-start(bf16[16,1,2,2048]{3,2,1,0:T(2,128)(2,1)} %bitcast.324), calls=%async_computation | async-start | bytes 262144 | tf_op jit(solution)/shard_map/while/body/eval_jaxpr/all_to_all | solution.py:118
  124.0 10.9 %all-to-all-start.1 = ((bf16[16,1,2,2048]{3,2,1,0:T(2,128)(2,1)}), bf16[16,1,2,2048]{3,2,1,0:T(2,128)(2,1)S(1)}, u32[]{:S(2)}, u32[]{:S(2)}) async-start(bf16[16,1,2,2048]{3,2,1,0:T(2,128)(2,1)} %copy.84), calls=%async_computation.1 | async-start | bytes 262144 | tf_op jit(solution)/shard_map/while/body/eval_jaxpr/all_to_all | solution.py:101
  135.2 6.2 collective-permute-start
  145.2 10.9 %all-to-all-start = ((bf16[16,1,2,2048]{3,2,1,0:T(2,128)(2,1)}), bf16[16,1,2,2048]{3,2,1,0:T(2,128)(2,1)S(1)}, u32[]{:S(2)}, u32[]{:S(2)}) async-start(bf16[16,1,2,2048]{3,2,1,0:T(2,128)(2,1)} %bitcast.324), calls=%async_computation | async-start | bytes 262144 | tf_op jit(solution)/shard_map/while/body/eval_jaxpr/all_to_all | solution.py:118
  160.3 10.9 %all-to-all-start.1 = ((bf16[16,1,2,2048]{3,2,1,0:T(2,128)(2,1)}), bf16[16,1,2,2048]{3,2,1,0:T(2,128)(2,1)S(1)}, u32[]{:S(2)}, u32[]{:S(2)}) async-start(bf16[16,1,2,2048]{3,2,1,0:T(2,128)(2,1)} %copy.84), calls=%async_computation.1 | async-start | bytes 262144 | tf_op jit(solution)/shard_map/while/body/eval_jaxpr/all_to_all | solution.py:101
  171.6 6.2 collective-permute-start
  181.5 10.9 %all-to-all-start = ((bf16[16,1,2,2048]{3,2,1,0:T(2,128)(2,1)}), bf16[16,1,2,2048]{3,2,1,0:T(2,128)(2,1)S(1)}, u32[]{:S(2)}, u32[]{:S(2)}) async-start(bf16[16,1,2,2048]{3,2,1,0:T(2,128)(2,1)} %bitcast.324), calls=%async_computation | async-start | bytes 262144 | tf_op jit(solution)/shard_map/while/body/eval_jaxpr/all_to_all | solution.py:118
  196.6 10.9 %all-to-all-start.1 = ((bf16[16,1,2,2048]{3,2,1,0:T(2,128)(2,1)}), bf16[16,1,2,2048]{3,2,1,0:T(2,128)(2,1)S(1)}, u32[]{:S(2)}, u32[]{:S(2)}) async-start(bf16[16,1,2,2048]{3,2,1,0:T(2,128)(2,1)} %copy.84), calls=%async_computation.1 | async-start | bytes 262144 | tf_op jit(solution)/shard_map/while/body/eval_jaxpr/all_to_all | solution.py:101
  207.9 6.2 collective-permute-start
  217.8 10.9 %all-to-all-start = ((bf16[16,1,2,2048]{3,2,1,0:T(2,128)(2,1)}), bf16[16,1,2,2048]{3,2,1,0:T(2,128)(2,1)S(1)}, u32[]{:S(2)}, u32[]{:S(2)}) async-start(bf16[16,1,2,2048]{3,2,1,0:T(2,128)(2,1)} %bitcast.324), calls=%async_computation | async-start | bytes 262144 | tf_op jit(solution)/shard_map/while/body/eval_jaxpr/all_to_all | solution.py:118
  233.0 10.9 %all-to-all-start.1 = ((bf16[16,1,2,2048]{3,2,1,0:T(2,128)(2,1)}), bf16[16,1,2,2048]{3,2,1,0:T(2,128)(2,1)S(1)}, u32[]{:S(2)}, u32[]{:S(2)}) async-start(bf16[16,1,2,2048]{3,2,1,0:T(2,128)(2,1)} %copy.84), calls=%async_computation.1 | async-start | bytes 262144 | tf_op jit(solution)/shard_map/while/body/eval_jaxpr/all_to_all | solution.py:101
  244.2 6.2 collective-permute-start
  254.1 10.9 %all-to-all-start = ((bf16[16,1,2,2048]{3,2,1,0:T(2,128)(2,1)}), bf16[16,1,2,2048]{3,2,1,0:T(2,128)(2,1)S(1)}, u32[]{:S(2)}, u32[]{:S(2)}) async-start(bf16[16,1,2,2048]{3,2,1,0:T(2,128)(2,1)} %bitcast.324), calls=%async_computation | async-start | bytes 262144 | tf_op jit(solution)/shard_map/while/body/eval_jaxpr/all_to_all | solution.py:118
  269.3 10.9 %all-to-all-start.1 = ((bf16[16,1,2,2048]{3,2,1,0:T(2,128)(2,1)}), bf16[16,1,2,2048]{3,2,1,0:T(2,128)(2,1)S(1)}, u32[]{:S(2)}, u32[]{:S(2)}) async-start(bf16[16,1,2,2048]{3,2,1,0:T(2,128)(2,1)} %copy.84), calls=%async_computation.1 | async-start | bytes 262144 | tf_op jit(solution)/shard_map/while/body/eval_jaxpr/all_to_all | solution.py:101
  280.5 6.2 collective-permute-start
  290.5 10.9 %all-to-all-start = ((bf16[16,1,2,2048]{3,2,1,0:T(2,128)(2,1)}), bf16[16,1,2,2048]{3,2,1,0:T(2,128)(2,1)S(1)}, u32[]{:S(2)}, u32[]{:S(2)}) async-start(bf16[16,1,2,2048]{3,2,1,0:T(2,128)(2,1)} %bitcast.324), calls=%async_computation | async-start | bytes 262144 | tf_op jit(solution)/shard_map/while/body/eval_jaxpr/all_to_all | solution.py:118
  305.6 10.9 %all-to-all-start.1 = ((bf16[16,1,2,2048]{3,2,1,0:T(2,128)(2,1)}), bf16[16,1,2,2048]{3,2,1,0:T(2,128)(2,1)S(1)}, u32[]{:S(2)}, u32[]{:S(2)}) async-start(bf16[16,1,2,2048]{3,2,1,0:T(2,128)(2,1)} %copy.84), calls=%async_computation.1 | async-start | bytes 262144 | tf_op jit(solution)/shard_map/while/body/eval_jaxpr/all_to_all | solution.py:101
  316.8 6.2 collective-permute-start
  326.8 10.9 %all-to-all-start = ((bf16[16,1,2,2048]{3,2,1,0:T(2,128)(2,1)}), bf16[16,1,2,2048]{3,2,1,0:T(2,128)(2,1)S(1)}, u32[]{:S(2)}, u32[]{:S(2)}) async-start(bf16[16,1,2,2048]{3,2,1,0:T(2,128)(2,1)} %bitcast.324), calls=%async_computation | async-start | bytes 262144 | tf_op jit(solution)/shard_map/while/body/eval_jaxpr/all_to_all | solution.py:118
  341.9 10.9 %all-to-all-start.1 = ((bf16[16,1,2,2048]{3,2,1,0:T(2,128)(2,1)}), bf16[16,1,2,2048]{3,2,1,0:T(2,128)(2,1)S(1)}, u32[]{:S(2)}, u32[]{:S(2)}) async-start(bf16[16,1,2,2048]{3,2,1,0:T(2,128)(2,1)} %copy.84), calls=%async_computation.1 | async-start | bytes 262144 | tf_op jit(solution)/shard_map/while/body/eval_jaxpr/all_to_all | solution.py:101
  353.2 6.2 collective-permute-start
  369.7 12.5 %all-to-all-start.2 = ((bf16[16,1,2,2048]{3,2,1,0:T(2,128)(2,1)}), bf16[16,1,2,2048]{3,2,1,0:T(2,128)(2,1)S(1)}, u32[]{:S(2)}, u32[]{:S(2)}) async-start(bf16[16,1,2,2048]{3,2,1,0:T(2,128)(2,1)} %bitcast.359), calls=%async_computation.2 | async-start | bytes 262144 | tf_op jit(solution)/shard_map/while/body/eval_jaxpr/all_to_all | solution.py:162
  387.4 12.0 %all-to-all-start.3 = ((bf16[16,1,2,2048]{3,2,1,0:T(2,128)(2,1)}), bf16[16,1,2,2048]{3,2,1,0:T(2,128)(2,1)S(1)}, u32[]{:S(2)}, u32[]{:S(2)}) async-start(bf16[16,1,2,2048]{3,2,1,0:T(2,128)(2,1)} %copy.87), calls=%async_computation.3 | async-start | bytes 262144 | tf_op jit(solution)/shard_map/while/body/eval_jaxpr/all_to_all | solution.py:167
  402.2 6.1 collective-permute-start.1
  414.5 12.6 %all-to-all-start.2 = ((bf16[16,1,2,2048]{3,2,1,0:T(2,128)(2,1)}), bf16[16,1,2,2048]{3,2,1,0:T(2,128)(2,1)S(1)}, u32[]{:S(2)}, u32[]{:S(2)}) async-start(bf16[16,1,2,2048]{3,2,1,0:T(2,128)(2,1)} %bitcast.359), calls=%async_computation.2 | async-start | bytes 262144 | tf_op jit(solution)/shard_map/while/body/eval_jaxpr/all_to_all | solution.py:162
  432.2 12.0 %all-to-all-start.3 = ((bf16[16,1,2,2048]{3,2,1,0:T(2,128)(2,1)}), bf16[16,1,2,2048]{3,2,1,0:T(2,128)(2,1)S(1)}, u32[]{:S(2)}, u32[]{:S(2)}) async-start(bf16[16,1,2,2048]{3,2,1,0:T(2,128)(2,1)} %copy.87), calls=%async_computation.3 | async-start | bytes 262144 | tf_op jit(solution)/shard_map/while/body/eval_jaxpr/all_to_all | solution.py:167
  447.1 6.1 collective-permute-start.1
  453.3 18.3 %copy-start.7 = (f32[16]{0:T(128)}, f32[16]{0:T(128)S(1)}, u32[]{:S(2)}) copy-start(f32[16]{0:T(128)S(1)} %add_rsqrt_fusion.5) | copy-start | bytes 196 | tf_op jit(solution)/shard_map/while
  459.4 12.6 %all-to-all-start.2 = ((bf16[16,1,2,2048]{3,2,1,0:T(2,128)(2,1)}), bf16[16,1,2,2048]{3,2,1,0:T(2,128)(2,1)S(1)}, u32[]{:S(2)}, u32[]{:S(2)}) async-start(bf16[16,1,2,2048]{3,2,1,0:T(2,128)(2,1)} %bitcast.359), calls=%async_computation.2 | async-start | bytes 262144 | tf_op jit(solution)/shard_map/while/body/eval_jaxpr/all_to_all | solution.py:162
  477.1 12.0 %all-to-all-start.3 = ((bf16[16,1,2,2048]{3,2,1,0:T(2,128)(2,1)}), bf16[16,1,2,2048]{3,2,1,0:T(2,128)(2,1)S(1)}, u32[]{:S(2)}, u32[]{:S(2)}) async-start(bf16[16,1,2,2048]{3,2,1,0:T(2,128)(2,1)} %copy.87), calls=%async_computation.3 | async-start | bytes 262144 | tf_op jit(solution)/shard_map/while/body/eval_jaxpr/all_to_all | solution.py:167
  491.9 6.1 collective-permute-start.1
  504.3 12.6 %all-to-all-start.2 = ((bf16[16,1,2,2048]{3,2,1,0:T(2,128)(2,1)}), bf16[16,1,2,2048]{3,2,1,0:T(2,128)(2,1)S(1)}, u32[]{:S(2)}, u32[]{:S(2)}) async-start(bf16[16,1,2,2048]{3,2,1,0:T(2,128)(2,1)} %bitcast.359), calls=%async_computation.2 | async-start | bytes 262144 | tf_op jit(solution)/shard_map/while/body/eval_jaxpr/all_to_all | solution.py:162
  522.0 12.0 %all-to-all-start.3 = ((bf16[16,1,2,2048]{3,2,1,0:T(2,128)(2,1)}), bf16[16,1,2,2048]{3,2,1,0:T(2,128)(2,1)S(1)}, u32[]{:S(2)}, u32[]{:S(2)}) async-start(bf16[16,1,2,2048]{3,2,1,0:T(2,128)(2,1)} %copy.87), calls=%async_computation.3 | async-start | bytes 262144 | tf_op jit(solution)/shard_map/while/body/eval_jaxpr/all_to_all | solution.py:167
  536.8 6.1 collective-permute-start.1
  543.1 18.3 %copy-start.7 = (f32[16]{0:T(128)}, f32[16]{0:T(128)S(1)}, u32[]{:S(2)}) copy-start(f32[16]{0:T(128)S(1)} %add_rsqrt_fusion.5) | copy-start | bytes 196 | tf_op jit(solution)/shard_map/while
  549.2 12.6 %all-to-all-start.2 = ((bf16[16,1,2,2048]{3,2,1,0:T(2,128)(2,1)}), bf16[16,1,2,2048]{3,2,1,0:T(2,128)(2,1)S(1)}, u32[]{:S(2)}, u32[]{:S(2)}) async-start(bf16[16,1,2,2048]{3,2,1,0:T(2,128)(2,1)} %bitcast.359), calls=%async_computation.2 | async-start | bytes 262144 | tf_op jit(solution)/shard_map/while/body/eval_jaxpr/all_to_all | solution.py:162
  566.9 12.0 %all-to-all-start.3 = ((bf16[16,1,2,2048]{3,2,1,0:T(2,128)(2,1)}), bf16[16,1,2,2048]{3,2,1,0:T(2,128)(2,1)S(1)}, u32[]{:S(2)}, u32[]{:S(2)}) async-start(bf16[16,1,2,2048]{3,2,1,0:T(2,128)(2,1)} %copy.87), calls=%async_computation.3 | async-start | bytes 262144 | tf_op jit(solution)/shard_map/while/body/eval_jaxpr/all_to_all | solution.py:167
  581.7 6.1 collective-permute-start.1
  594.0 12.6 %all-to-all-start.2 = ((bf16[16,1,2,2048]{3,2,1,0:T(2,128)(2,1)}), bf16[16,1,2,2048]{3,2,1,0:T(2,128)(2,1)S(1)}, u32[]{:S(2)}, u32[]{:S(2)}) async-start(bf16[16,1,2,2048]{3,2,1,0:T(2,128)(2,1)} %bitcast.359), calls=%async_computation.2 | async-start | bytes 262144 | tf_op jit(solution)/shard_map/while/body/eval_jaxpr/all_to_all | solution.py:162
  611.7 12.0 %all-to-all-start.3 = ((bf16[16,1,2,2048]{3,2,1,0:T(2,128)(2,1)}), bf16[16,1,2,2048]{3,2,1,0:T(2,128)(2,1)S(1)}, u32[]{:S(2)}, u32[]{:S(2)}) async-start(bf16[16,1,2,2048]{3,2,1,0:T(2,128)(2,1)} %copy.87), calls=%async_computation.3 | async-start | bytes 262144 | tf_op jit(solution)/shard_map/while/body/eval_jaxpr/all_to_all | solution.py:167
  626.5 6.1 collective-permute-start.1
  632.8 18.3 %copy-start.7 = (f32[16]{0:T(128)}, f32[16]{0:T(128)S(1)}, u32[]{:S(2)}) copy-start(f32[16]{0:T(128)S(1)} %add_rsqrt_fusion.5) | copy-start | bytes 196 | tf_op jit(solution)/shard_map/while
  638.9 12.6 %all-to-all-start.2 = ((bf16[16,1,2,2048]{3,2,1,0:T(2,128)(2,1)}), bf16[16,1,2,2048]{3,2,1,0:T(2,128)(2,1)S(1)}, u32[]{:S(2)}, u32[]{:S(2)}) async-start(bf16[16,1,2,2048]{3,2,1,0:T(2,128)(2,1)} %bitcast.359), calls=%async_computation.2 | async-start | bytes 262144 | tf_op jit(solution)/shard_map/while/body/eval_jaxpr/all_to_all | solution.py:162
  656.6 12.0 %all-to-all-start.3 = ((bf16[16,1,2,2048]{3,2,1,0:T(2,128)(2,1)}), bf16[16,1,2,2048]{3,2,1,0:T(2,128)(2,1)S(1)}, u32[]{:S(2)}, u32[]{:S(2)}) async-start(bf16[16,1,2,2048]{3,2,1,0:T(2,128)(2,1)} %copy.87), calls=%async_computation.3 | async-start | bytes 262144 | tf_op jit(solution)/shard_map/while/body/eval_jaxpr/all_to_all | solution.py:167
  671.4 6.1 collective-permute-start.1
  677.7 18.3 %copy-start.7 = (f32[16]{0:T(128)}, f32[16]{0:T(128)S(1)}, u32[]{:S(2)}) copy-start(f32[16]{0:T(128)S(1)} %add_rsqrt_fusion.5) | copy-start | bytes 196 | tf_op jit(solution)/shard_map/while
  683.8 12.6 %all-to-all-start.2 = ((bf16[16,1,2,2048]{3,2,1,0:T(2,128)(2,1)}), bf16[16,1,2,2048]{3,2,1,0:T(2,128)(2,1)S(1)}, u32[]{:S(2)}, u32[]{:S(2)}) async-start(bf16[16,1,2,2048]{3,2,1,0:T(2,128)(2,1)} %bitcast.359), calls=%async_computation.2 | async-start | bytes 262144 | tf_op jit(solution)/shard_map/while/body/eval_jaxpr/all_to_all | solution.py:162
  701.5 12.0 %all-to-all-start.3 = ((bf16[16,1,2,2048]{3,2,1,0:T(2,128)(2,1)}), bf16[16,1,2,2048]{3,2,1,0:T(2,128)(2,1)S(1)}, u32[]{:S(2)}, u32[]{:S(2)}) async-start(bf16[16,1,2,2048]{3,2,1,0:T(2,128)(2,1)} %copy.87), calls=%async_computation.3 | async-start | bytes 262144 | tf_op jit(solution)/shard_map/while/body/eval_jaxpr/all_to_all | solution.py:167
  716.3 6.1 collective-permute-start.1
  728.7 12.6 %all-to-all-start.2 = ((bf16[16,1,2,2048]{3,2,1,0:T(2,128)(2,1)}), bf16[16,1,2,2048]{3,2,1,0:T(2,128)(2,1)S(1)}, u32[]{:S(2)}, u32[]{:S(2)}) async-start(bf16[16,1,2,2048]{3,2,1,0:T(2,128)(2,1)} %bitcast.359), calls=%async_computation.2 | async-start | bytes 262144 | tf_op jit(solution)/shard_map/while/body/eval_jaxpr/all_to_all | solution.py:162
  746.4 12.0 %all-to-all-start.3 = ((bf16[16,1,2,2048]{3,2,1,0:T(2,128)(2,1)}), bf16[16,1,2,2048]{3,2,1,0:T(2,128)(2,1)S(1)}, u32[]{:S(2)}, u32[]{:S(2)}) async-start(bf16[16,1,2,2048]{3,2,1,0:T(2,128)(2,1)} %copy.87), calls=%async_computation.3 | async-start | bytes 262144 | tf_op jit(solution)/shard_map/while/body/eval_jaxpr/all_to_all | solution.py:167
  761.2 6.1 collective-permute-start.1
  768.0 89.0 %reduce-scatter.2.cloned.1.call-start = ((), (), s32[]{:S(2)}) async-start(), calls=%async_computation.5 | async-start | bytes 786432 | tf_op jit(solution)/shard_map/reduce_scatter | solution.py:227
  770.1 39.0 %copy-start.3 = (bf16[8,16,1,2,2048]{4,3,1,2,0:T(2,128)(2,1)S(1)}, bf16[8,16,1,2,2048]{4,3,1,2,0:T(2,128)(2,1)}, u32[]{:S(2)}) copy-start(bf16[8,16,1,2,2048]{4,3,1,2,0:T(2,128)(2,1)} %get-tuple-element.697) | copy-start | bytes 3145732
  770.1 39.0 %copy-start.5 = (bf16[8,16,1,2,512]{4,1,3,2,0:T(8,128)(2,1)S(1)}, bf16[8,16,1,2,512]{4,1,3,2,0:T(8,128)(2,1)}, u32[]{:S(2)}) copy-start(bf16[8,16,1,2,512]{4,1,3,2,0:T(8,128)(2,1)} %get-tuple-element.696) | copy-start | bytes 786436
  (24 other events, 323.2 us)
Sparse Core Ops, SparseCore 0:
  768.1 87.3 all-reduce.1
Sparse Core Ops, SparseCore 1:
  771.3 13.1 reduce-scatter.1
where the time goes:
time: 874 us; the launch traced here: 864 us
  starting transfers between devices  235 us (27%)
  waiting for transfers between devices  194 us (22%)
  matrix products  157 us (18%)
  other arithmetic  119 us (14%)
  local copies, waits for them, and re-layouts  90.7 us (10%)
  blocking collectives  51.6 us (6%)
  between operations  15.6 us (2%)
    dynamic_update_slice x63, other arithmetic, keep_row(): lax.dynamic_update_index_in_dim(stash, jnp.where(active, value, old_row),...  67.9 us
    all_to_all x9, starting transfers between devices, backward_tick(): lax.all_to_all(rows_grad, ('expert', 'dp'), split_axis=0, concat_axis=0,...  54.7 us
    dot_general x18, matrix products, expert_inner(): jnp.einsum('sekd,edf->sekf', exp_rows, w_gu, preferred_element_type=jnp.f...  54.1 us
    ppermute x18, starting transfers between devices, shifted(): lax.ppermute(value, axis, [(source, source + steps) for source in range(l...  49.1 us
    all_to_all x9, waiting for transfers between devices, expert_forward(): lax.all_to_all(out_rows, ('expert', 'dp'), split_axis=0, concat_axis=0, t...  47.7 us
    all_to_all x9, starting transfers between devices, forward_tick(): lax.all_to_all(send_rows, ('expert', 'dp'), split_axis=0, concat_axis=0,...  44.6 us
    psum x1, waiting for transfers between devices, local(): lax.psum(acc_router.astype(jnp.bfloat16), ('expert', 'dp'))  43.3 us
    all_to_all x9, starting transfers between devices, backward_tick(): lax.all_to_all(dy_send, ('expert', 'dp'), split_axis=0, concat_axis=0, ti...  43.3 us
  transfers between devices with their start and end apart: 56, of which 46 were waited for; matrix products, arithmetic and copies ran while one was open for 18% of the time, Pallas kernels for 0%

commit v1 on v0

--- a/solution.py
+++ b/solution.py
@@ -4,6 +4,28 @@
 from jax.sharding import PartitionSpec as P
 
 EPS = 1e-05
+
+
+def in_blocks(array, dim, length):
+    before, after = (array.shape[:dim], array.shape[dim + 1 :])
+    return jnp.moveaxis(array.reshape(*before, length, -1, *after), dim, 0)
+
+
+def laid_out(pieces, dim):
+    pieces = jnp.moveaxis(pieces, 0, dim)
+    dims = pieces.shape
+    return pieces.reshape(*dims[:dim], dims[dim] * dims[dim + 1], *dims[dim + 2 :])
+
+
+def exchange_in_pairs(value, axis, split_dim, concat_dim):
+    peers, here = (lax.axis_size(axis), lax.axis_index(axis))
+    blocks = in_blocks(value, split_dim, peers)
+    gathered = [blocks[here]]
+    for step in range(1, peers):
+        sent = blocks[here ^ step]
+        gathered.append(lax.ppermute(sent, axis, [(i, i ^ step) for i in range(peers)]))
+    blocks = jnp.stack(gathered)[here ^ jnp.arange(peers)]
+    return laid_out(blocks, concat_dim)
 
 
 def shifted(value, axis, steps):
@@ -114,9 +136,7 @@
         expert_hits, slot_place = slot_tables(route_rows, n_expert, capacity)
         send_rows = jnp.einsum("ktc,td->cd", slot_place, normed, preferred_element_type=jnp.float32)
         send_rows = send_rows.astype(jnp.bfloat16).reshape(rows_shape)
-        returned, landed = expert_forward(
-            lax.all_to_all(send_rows, ("expert", "dp"), split_axis=0, concat_axis=0, tiled=True)
-        )
+        returned, landed = expert_forward(exchange_in_pairs(send_rows, ("expert", "dp"), 0, 0))
         back_flat = returned.reshape(cells, model_width)
         picked = jnp.einsum(
             "ktc,cd->ktd", slot_place, back_flat, preferred_element_type=jnp.float32

time: 874 us -> 1020 us (1.17)
  starting transfers between devices: 235 us -> 389 us
    ppermute x0 -> x135, starting transfers between devices: none -> 177 us  [exchange_in_pairs(): lax.ppermute(sent, axis, [(i, i ^ step) for i in range(peers)])]
    all_to_all x9 -> x0, starting transfers between devices: 44.6 us -> none  [forward_tick(): lax.all_to_all(send_rows, ('expert', 'dp'), split_axis=0, concat_axis=0,...]
    all_to_all x9 -> x0, waiting for transfers between devices: 34.5 us -> none  [forward_tick(): lax.all_to_all(send_rows, ('expert', 'dp'), split_axis=0, concat_axis=0,...]
    ppermute x0 -> x135, waiting for transfers between devices: none -> 33.9 us  [exchange_in_pairs(): lax.ppermute(sent, axis, [(i, i ^ step) for i in range(peers)])]
    all_to_all x9, starting transfers between devices: 43.1 us -> 64.6 us  [expert_forward(): lax.all_to_all(out_rows, ('expert', 'dp'), split_axis=0, concat_axis=0, t...]
    dynamic_slice x45 -> x36, local copies, waits for them, and re-layouts: 32.7 us -> 23.6 us  [keep_row(): old_row = lax.dynamic_index_in_dim(stash, position, 0, keepdims=False)]
  transfers between devices with their start and end apart: 56 -> 182, of which waited for: 46 -> 55; matrix products, arithmetic and copies ran while one was open for 18% -> 16% of each run, Pallas kernels for 0% -> 0%
where the time goes in v1:
time: 1020 us
  starting transfers between devices  389 us (38%)
  waiting for transfers between devices  184 us (18%)
  matrix products  157 us (15%)
  other arithmetic  128 us (13%)
  local copies, waits for them, and re-layouts  86.4 us (8%)
  blocking collectives  51.6 us (5%)
  between operations  15.6 us (2%)
    ppermute x135, starting transfers between devices, exchange_in_pairs(): lax.ppermute(sent, axis, [(i, i ^ step) for i in range(peers)])  177 us
    dynamic_update_slice x63, other arithmetic, keep_row(): lax.dynamic_update_index_in_dim(stash, jnp.where(active, value, old_row),...  76 us
    all_to_all x9, starting transfers between devices, expert_forward(): lax.all_to_all(out_rows, ('expert', 'dp'), split_axis=0, concat_axis=0, t...  64.6 us
    all_to_all x9, starting transfers between devices, backward_tick(): lax.all_to_all(rows_grad, ('expert', 'dp'), split_axis=0, concat_axis=0,...  54.7 us
    dot_general x18, matrix products, expert_inner(): jnp.einsum('sekd,edf->sekf', exp_rows, w_gu, preferred_element_type=jnp.f...  54.2 us
    ppermute x18, starting transfers between devices, shifted(): lax.ppermute(value, axis, [(source, source + steps) for source in range(l...  49.1 us
    all_to_all x9, starting transfers between devices, backward_tick(): lax.all_to_all(dy_send, ('expert', 'dp'), split_axis=0, concat_axis=0, ti...  43.3 us
    psum x1, waiting for transfers between devices, local(): lax.psum(acc_router.astype(jnp.bfloat16), ('expert', 'dp'))  43.2 us
  transfers between devices with their start and end apart: 182, of which 55 were waited for; matrix products, arithmetic and copies ran while one was open for 16% of the time, Pallas kernels for 0%

profile of v1, /device:TPU:8, one launch (start us, length us, event | category | flops | bytes accessed | tf_op | source)
XLA Modules:
  0.0 1015.4 jit_solution(10446950949976263124)
XLA Ops:
  8.1 10.6 %all_gather.6 = bf16[8,16,2048]{2,1,0:T(8,128)(2,1)} all-gather(bf16[8,16,1024]{2,1,0:T(8,128)(2,1)} %param.12), channel_id=1, replica_groups=mesh['section'=2,'expert'=4,'dp'=4] {'section'}, dimensions={2}, use_global_device_ids=true | all-gather | bytes 786432 | tf_op jit(solution)/shard_map/all_gather | solution.py:107
  18.6 8.9 all_gather.7
  31.9 478.4 %while.48 = (s32[]{:T(128)}, bf16[16,2048]{1,0:T(8,128)(2,1)S(1)}, bf16[8,16,2048]{2,1,0:T(8,128)(2,1)S(1)}, bf16[8,32,2048]{2,1,0:T(8,128)(2,1)}, bf16[8,16,1,2...) while((s32[]{:T(128)}, bf16[16,2048]{1,0:T(8,128)(2,1)S(1)}, ...), condition=%wide.region_7.8_spmd, body=%wide.region_0.7_spmd.sunk | while | flops 209599520 | bytes 12242162 | solution.py:160
  65.7 6.6 all-to-all-start
  74.0 4.4 all-to-all-done
  102.7 4.7 collective-permute-start.12
  117.5 7.3 all-to-all-start
  126.5 4.3 all-to-all-done
  131.1 4.3 collective-permute-start.15
  156.0 4.7 collective-permute-start.12
  170.8 7.3 all-to-all-start
  179.8 4.3 all-to-all-done
  184.4 4.3 collective-permute-start.15
  209.3 4.7 collective-permute-start.12
  224.1 7.3 all-to-all-start
  233.0 4.3 all-to-all-done
  237.7 4.3 collective-permute-start.15
  262.6 4.7 collective-permute-start.12
  277.4 7.3 all-to-all-start
  286.3 4.3 all-to-all-done
  291.0 4.3 collective-permute-start.15
  315.9 4.7 collective-permute-start.12
  330.7 7.3 all-to-all-start
  339.6 4.3 all-to-all-done
  344.3 4.3 collective-permute-start.15
  369.2 4.7 collective-permute-start.12
  384.0 7.3 all-to-all-start
  392.9 4.3 all-to-all-done
  397.5 4.3 collective-permute-start.15
  422.5 4.7 collective-permute-start.12
  437.2 7.3 all-to-all-start
  446.2 4.3 all-to-all-done
  450.8 4.3 collective-permute-start.15
  475.8 4.7 collective-permute-start.12
  490.5 7.3 all-to-all-start
  499.5 4.3 all-to-all-done
  504.1 4.3 collective-permute-start.15
  514.4 403.9 %while.49 = (s32[]{:T(128)}, bf16[16,2048]{1,0:T(8,128)(2,1)S(1)}, bf16[8,16,1,2,2048]{4,3,1,2,0:T(2,128)(2,1)}, bf16[8,16,1,2,512]{4,1,3,2,0:T(8,128)(2,1)}, bf...) while((s32[]{:T(128)}, bf16[16,2048]{1,0:T(8,128)(2,1)S(1)}, ...), condition=%wide.region_18.19_spmd.clone, body=%wide.region_8.18_spmd.clone.sunk | while | flops 361911744 | bytes 17806364 | solution.py:234
  520.6 4.8 all-to-all-start.1
  538.3 6.1 all-to-all-start.2
  546.7 3.7 all-to-all-done.2
  555.1 4.2 collective-permute-done.16
  565.5 4.8 all-to-all-start.1
  583.2 6.1 all-to-all-start.2
  591.6 3.7 all-to-all-done.2
  610.4 4.8 all-to-all-start.1
  628.1 6.1 all-to-all-start.2
  655.3 4.8 all-to-all-start.1
  673.0 6.1 all-to-all-start.2
  681.3 3.7 all-to-all-done.2
  700.1 4.8 all-to-all-start.1
  717.8 6.1 all-to-all-start.2
  745.0 4.8 all-to-all-start.1
  762.7 6.1 all-to-all-start.2
  789.9 4.8 all-to-all-start.1
  807.6 6.1 all-to-all-start.2
  815.9 3.7 all-to-all-done.2
  834.8 4.8 all-to-all-start.1
  852.5 6.1 all-to-all-start.2
  879.7 4.8 all-to-all-start.1
  897.3 6.1 all-to-all-start.2
  921.2 6.2 convolution_bitcast_fusion.1
  927.5 32.1 %psum.15 = bf16[1,2048]{1,0:T(2,128)(2,1)S(1)} all-reduce(bf16[1,2048]{1,0:T(2,128)(2,1)S(1)} %broadcast_in_dim.180), channel_id=1, replica_groups=mesh['section'=2,'expert'=4,'dp'=4] {'expert','dp'}, use_global_device_ids=true, to_apply=%region_21.22 | all-reduce | flops 2048 | bytes 8192 | tf_op jit(solution)/shard_map/psum | solution.py:244
  963.2 43.2 %all-reduce.2.cloned.1.call-done = bf16[1,2048,16]{1,2,0:T(8,128)(2,1)} async-done(((bf16[1,2048,16]{1,2,0:T(8,128)(2,1)}), bf16[1,2048,16]{1,2,0:T(8,128)(2,1)}) %all-reduce.2.cloned.1.call-update) | async-done | bytes 65552 | tf_op jit(solution)/shard_map/psum | solution.py:243
  (1111 shorter events, 603.0 us)
Async XLA Ops:
  8.0 998.4 %all-reduce.2.cloned.1.call-start = ((), (), s32[]{:S(2)}) async-start(), calls=%async_computation.5 | async-start | bytes 131072 | tf_op jit(solution)/shard_map/psum | solution.py:243
  35.4 8.4 collective-permute-start.1
  38.9 8.4 collective-permute-start.4
  41.4 8.4 collective-permute-start.5
  45.7 8.5 collective-permute-start.8
  47.3 9.3 collective-permute-start.9
  65.7 12.6 %all-to-all-start = ((bf16[16,1,2,2048]{3,2,1,0:T(2,128)(2,1)}), bf16[16,1,2,2048]{3,2,1,0:T(2,128)(2,1)S(1)}, u32[]{:S(2)}, u32[]{:S(2)}) async-start(bf16[16,1,2,2048]{3,2,1,0:T(2,128)(2,1)} %copy.81), calls=%async_computation | async-start | bytes 262144 | tf_op jit(solution)/shard_map/while/body/eval_jaxpr/all_to_all | solution.py:123
  90.9 9.7 collective-permute-start.4
  96.9 10.5 %collective-permute-start.8 = (bf16[1,1,2,2048]{3,2,1,0:T(2,128)(2,1)S(1)}, bf16[1,1,2,2048]{3,2,1,0:T(2,128)(2,1)S(1)}, u32[]{:S(2)}, u32[]{:S(2)}) collective-permute-start(bf16[1,1,2,2048]{3,2,1,0:T(2,128)(2,1)S(1)} %get-tuple-element.1152), channel_id=1, source_target_pairs={{0,9},{1,8},{2,11},{3,10},{4,13},{5,12},{6,15},{7,14},{8,1},{9,0},... | collective-permute-start | bytes 24584 | tf_op jit(solution)/shard_map/while/body/eval_jaxpr/ppermute | solution.py:26
  100.7 7.8 collective-permute-start.10
  117.5 13.2 %all-to-all-start = ((bf16[16,1,2,2048]{3,2,1,0:T(2,128)(2,1)}), bf16[16,1,2,2048]{3,2,1,0:T(2,128)(2,1)S(1)}, u32[]{:S(2)}, u32[]{:S(2)}) async-start(bf16[16,1,2,2048]{3,2,1,0:T(2,128)(2,1)} %copy.81), calls=%async_computation | async-start | bytes 262144 | tf_op jit(solution)/shard_map/while/body/eval_jaxpr/all_to_all | solution.py:123
  144.2 9.7 collective-permute-start.4
  148.1 7.8 collective-permute-start.6
  150.2 10.5 %collective-permute-start.8 = (bf16[1,1,2,2048]{3,2,1,0:T(2,128)(2,1)S(1)}, bf16[1,1,2,2048]{3,2,1,0:T(2,128)(2,1)S(1)}, u32[]{:S(2)}, u32[]{:S(2)}) collective-permute-start(bf16[1,1,2,2048]{3,2,1,0:T(2,128)(2,1)S(1)} %get-tuple-element.1152), channel_id=1, source_target_pairs={{0,9},{1,8},{2,11},{3,10},{4,13},{5,12},{6,15},{7,14},{8,1},{9,0},... | collective-permute-start | bytes 24584 | tf_op jit(solution)/shard_map/while/body/eval_jaxpr/ppermute | solution.py:26
  154.0 7.8 collective-permute-start.10
  170.8 13.2 %all-to-all-start = ((bf16[16,1,2,2048]{3,2,1,0:T(2,128)(2,1)}), bf16[16,1,2,2048]{3,2,1,0:T(2,128)(2,1)S(1)}, u32[]{:S(2)}, u32[]{:S(2)}) async-start(bf16[16,1,2,2048]{3,2,1,0:T(2,128)(2,1)} %copy.81), calls=%async_computation | async-start | bytes 262144 | tf_op jit(solution)/shard_map/while/body/eval_jaxpr/all_to_all | solution.py:123
  197.5 9.7 collective-permute-start.4
  201.4 7.8 collective-permute-start.6
  203.5 10.5 %collective-permute-start.8 = (bf16[1,1,2,2048]{3,2,1,0:T(2,128)(2,1)S(1)}, bf16[1,1,2,2048]{3,2,1,0:T(2,128)(2,1)S(1)}, u32[]{:S(2)}, u32[]{:S(2)}) collective-permute-start(bf16[1,1,2,2048]{3,2,1,0:T(2,128)(2,1)S(1)} %get-tuple-element.1152), channel_id=1, source_target_pairs={{0,9},{1,8},{2,11},{3,10},{4,13},{5,12},{6,15},{7,14},{8,1},{9,0},... | collective-permute-start | bytes 24584 | tf_op jit(solution)/shard_map/while/body/eval_jaxpr/ppermute | solution.py:26
  207.3 7.8 collective-permute-start.10
  224.1 13.2 %all-to-all-start = ((bf16[16,1,2,2048]{3,2,1,0:T(2,128)(2,1)}), bf16[16,1,2,2048]{3,2,1,0:T(2,128)(2,1)S(1)}, u32[]{:S(2)}, u32[]{:S(2)}) async-start(bf16[16,1,2,2048]{3,2,1,0:T(2,128)(2,1)} %copy.81), calls=%async_computation | async-start | bytes 262144 | tf_op jit(solution)/shard_map/while/body/eval_jaxpr/all_to_all | solution.py:123
  250.8 9.7 collective-permute-start.4
  254.7 7.8 collective-permute-start.6
  256.8 10.5 %collective-permute-start.8 = (bf16[1,1,2,2048]{3,2,1,0:T(2,128)(2,1)S(1)}, bf16[1,1,2,2048]{3,2,1,0:T(2,128)(2,1)S(1)}, u32[]{:S(2)}, u32[]{:S(2)}) collective-permute-start(bf16[1,1,2,2048]{3,2,1,0:T(2,128)(2,1)S(1)} %get-tuple-element.1152), channel_id=1, source_target_pairs={{0,9},{1,8},{2,11},{3,10},{4,13},{5,12},{6,15},{7,14},{8,1},{9,0},... | collective-permute-start | bytes 24584 | tf_op jit(solution)/shard_map/while/body/eval_jaxpr/ppermute | solution.py:26
  260.6 7.8 collective-permute-start.10
  277.4 13.2 %all-to-all-start = ((bf16[16,1,2,2048]{3,2,1,0:T(2,128)(2,1)}), bf16[16,1,2,2048]{3,2,1,0:T(2,128)(2,1)S(1)}, u32[]{:S(2)}, u32[]{:S(2)}) async-start(bf16[16,1,2,2048]{3,2,1,0:T(2,128)(2,1)} %copy.81), calls=%async_computation | async-start | bytes 262144 | tf_op jit(solution)/shard_map/while/body/eval_jaxpr/all_to_all | solution.py:123
  304.1 9.7 collective-permute-start.4
  308.0 7.8 collective-permute-start.6
  310.1 10.5 %collective-permute-start.8 = (bf16[1,1,2,2048]{3,2,1,0:T(2,128)(2,1)S(1)}, bf16[1,1,2,2048]{3,2,1,0:T(2,128)(2,1)S(1)}, u32[]{:S(2)}, u32[]{:S(2)}) collective-permute-start(bf16[1,1,2,2048]{3,2,1,0:T(2,128)(2,1)S(1)} %get-tuple-element.1152), channel_id=1, source_target_pairs={{0,9},{1,8},{2,11},{3,10},{4,13},{5,12},{6,15},{7,14},{8,1},{9,0},... | collective-permute-start | bytes 24584 | tf_op jit(solution)/shard_map/while/body/eval_jaxpr/ppermute | solution.py:26
  313.9 7.8 collective-permute-start.10
  330.7 13.2 %all-to-all-start = ((bf16[16,1,2,2048]{3,2,1,0:T(2,128)(2,1)}), bf16[16,1,2,2048]{3,2,1,0:T(2,128)(2,1)S(1)}, u32[]{:S(2)}, u32[]{:S(2)}) async-start(bf16[16,1,2,2048]{3,2,1,0:T(2,128)(2,1)} %copy.81), calls=%async_computation | async-start | bytes 262144 | tf_op jit(solution)/shard_map/while/body/eval_jaxpr/all_to_all | solution.py:123
  357.3 9.7 collective-permute-start.4
  361.2 7.8 collective-permute-start.6
  363.4 10.5 %collective-permute-start.8 = (bf16[1,1,2,2048]{3,2,1,0:T(2,128)(2,1)S(1)}, bf16[1,1,2,2048]{3,2,1,0:T(2,128)(2,1)S(1)}, u32[]{:S(2)}, u32[]{:S(2)}) collective-permute-start(bf16[1,1,2,2048]{3,2,1,0:T(2,128)(2,1)S(1)} %get-tuple-element.1152), channel_id=1, source_target_pairs={{0,9},{1,8},{2,11},{3,10},{4,13},{5,12},{6,15},{7,14},{8,1},{9,0},... | collective-permute-start | bytes 24584 | tf_op jit(solution)/shard_map/while/body/eval_jaxpr/ppermute | solution.py:26
  367.2 7.8 collective-permute-start.10
  384.0 13.2 %all-to-all-start = ((bf16[16,1,2,2048]{3,2,1,0:T(2,128)(2,1)}), bf16[16,1,2,2048]{3,2,1,0:T(2,128)(2,1)S(1)}, u32[]{:S(2)}, u32[]{:S(2)}) async-start(bf16[16,1,2,2048]{3,2,1,0:T(2,128)(2,1)} %copy.81), calls=%async_computation | async-start | bytes 262144 | tf_op jit(solution)/shard_map/while/body/eval_jaxpr/all_to_all | solution.py:123
  410.6 9.7 collective-permute-start.4
  414.5 7.8 collective-permute-start.6
  416.7 10.5 %collective-permute-start.8 = (bf16[1,1,2,2048]{3,2,1,0:T(2,128)(2,1)S(1)}, bf16[1,1,2,2048]{3,2,1,0:T(2,128)(2,1)S(1)}, u32[]{:S(2)}, u32[]{:S(2)}) collective-permute-start(bf16[1,1,2,2048]{3,2,1,0:T(2,128)(2,1)S(1)} %get-tuple-element.1152), channel_id=1, source_target_pairs={{0,9},{1,8},{2,11},{3,10},{4,13},{5,12},{6,15},{7,14},{8,1},{9,0},... | collective-permute-start | bytes 24584 | tf_op jit(solution)/shard_map/while/body/eval_jaxpr/ppermute | solution.py:26
  420.5 7.8 collective-permute-start.10
  437.2 13.2 %all-to-all-start = ((bf16[16,1,2,2048]{3,2,1,0:T(2,128)(2,1)}), bf16[16,1,2,2048]{3,2,1,0:T(2,128)(2,1)S(1)}, u32[]{:S(2)}, u32[]{:S(2)}) async-start(bf16[16,1,2,2048]{3,2,1,0:T(2,128)(2,1)} %copy.81), calls=%async_computation | async-start | bytes 262144 | tf_op jit(solution)/shard_map/while/body/eval_jaxpr/all_to_all | solution.py:123
  463.9 9.7 collective-permute-start.4
  467.8 7.8 collective-permute-start.6
  470.0 10.5 %collective-permute-start.8 = (bf16[1,1,2,2048]{3,2,1,0:T(2,128)(2,1)S(1)}, bf16[1,1,2,2048]{3,2,1,0:T(2,128)(2,1)S(1)}, u32[]{:S(2)}, u32[]{:S(2)}) collective-permute-start(bf16[1,1,2,2048]{3,2,1,0:T(2,128)(2,1)S(1)} %get-tuple-element.1152), channel_id=1, source_target_pairs={{0,9},{1,8},{2,11},{3,10},{4,13},{5,12},{6,15},{7,14},{8,1},{9,0},... | collective-permute-start | bytes 24584 | tf_op jit(solution)/shard_map/while/body/eval_jaxpr/ppermute | solution.py:26
  490.5 13.2 %all-to-all-start = ((bf16[16,1,2,2048]{3,2,1,0:T(2,128)(2,1)}), bf16[16,1,2,2048]{3,2,1,0:T(2,128)(2,1)S(1)}, u32[]{:S(2)}, u32[]{:S(2)}) async-start(bf16[16,1,2,2048]{3,2,1,0:T(2,128)(2,1)} %copy.81), calls=%async_computation | async-start | bytes 262144 | tf_op jit(solution)/shard_map/while/body/eval_jaxpr/all_to_all | solution.py:123
  520.6 12.6 %all-to-all-start.1 = ((bf16[16,1,2,2048]{3,2,1,0:T(2,128)(2,1)}), bf16[16,1,2,2048]{3,2,1,0:T(2,128)(2,1)S(1)}, u32[]{:S(2)}, u32[]{:S(2)}) async-start(bf16[16,1,2,2048]{3,2,1,0:T(2,128)(2,1)} %bitcast.444), calls=%async_computation.1 | async-start | bytes 262144 | tf_op jit(solution)/shard_map/while/body/eval_jaxpr/all_to_all | solution.py:182
  538.3 12.0 %all-to-all-start.2 = ((bf16[16,1,2,2048]{3,2,1,0:T(2,128)(2,1)}), bf16[16,1,2,2048]{3,2,1,0:T(2,128)(2,1)S(1)}, u32[]{:S(2)}, u32[]{:S(2)}) async-start(bf16[16,1,2,2048]{3,2,1,0:T(2,128)(2,1)} %copy.84), calls=%async_computation.2 | async-start | bytes 262144 | tf_op jit(solution)/shard_map/while/body/eval_jaxpr/all_to_all | solution.py:187
  565.5 12.6 %all-to-all-start.1 = ((bf16[16,1,2,2048]{3,2,1,0:T(2,128)(2,1)}), bf16[16,1,2,2048]{3,2,1,0:T(2,128)(2,1)S(1)}, u32[]{:S(2)}, u32[]{:S(2)}) async-start(bf16[16,1,2,2048]{3,2,1,0:T(2,128)(2,1)} %bitcast.444), calls=%async_computation.1 | async-start | bytes 262144 | tf_op jit(solution)/shard_map/while/body/eval_jaxpr/all_to_all | solution.py:182
  583.2 12.0 %all-to-all-start.2 = ((bf16[16,1,2,2048]{3,2,1,0:T(2,128)(2,1)}), bf16[16,1,2,2048]{3,2,1,0:T(2,128)(2,1)S(1)}, u32[]{:S(2)}, u32[]{:S(2)}) async-start(bf16[16,1,2,2048]{3,2,1,0:T(2,128)(2,1)} %copy.84), calls=%async_computation.2 | async-start | bytes 262144 | tf_op jit(solution)/shard_map/while/body/eval_jaxpr/all_to_all | solution.py:187
  610.4 12.6 %all-to-all-start.1 = ((bf16[16,1,2,2048]{3,2,1,0:T(2,128)(2,1)}), bf16[16,1,2,2048]{3,2,1,0:T(2,128)(2,1)S(1)}, u32[]{:S(2)}, u32[]{:S(2)}) async-start(bf16[16,1,2,2048]{3,2,1,0:T(2,128)(2,1)} %bitcast.444), calls=%async_computation.1 | async-start | bytes 262144 | tf_op jit(solution)/shard_map/while/body/eval_jaxpr/all_to_all | solution.py:182
  628.1 12.0 %all-to-all-start.2 = ((bf16[16,1,2,2048]{3,2,1,0:T(2,128)(2,1)}), bf16[16,1,2,2048]{3,2,1,0:T(2,128)(2,1)S(1)}, u32[]{:S(2)}, u32[]{:S(2)}) async-start(bf16[16,1,2,2048]{3,2,1,0:T(2,128)(2,1)} %copy.84), calls=%async_computation.2 | async-start | bytes 262144 | tf_op jit(solution)/shard_map/while/body/eval_jaxpr/all_to_all | solution.py:187
  655.3 12.6 %all-to-all-start.1 = ((bf16[16,1,2,2048]{3,2,1,0:T(2,128)(2,1)}), bf16[16,1,2,2048]{3,2,1,0:T(2,128)(2,1)S(1)}, u32[]{:S(2)}, u32[]{:S(2)}) async-start(bf16[16,1,2,2048]{3,2,1,0:T(2,128)(2,1)} %bitcast.444), calls=%async_computation.1 | async-start | bytes 262144 | tf_op jit(solution)/shard_map/while/body/eval_jaxpr/all_to_all | solution.py:182
  673.0 12.0 %all-to-all-start.2 = ((bf16[16,1,2,2048]{3,2,1,0:T(2,128)(2,1)}), bf16[16,1,2,2048]{3,2,1,0:T(2,128)(2,1)S(1)}, u32[]{:S(2)}, u32[]{:S(2)}) async-start(bf16[16,1,2,2048]{3,2,1,0:T(2,128)(2,1)} %copy.84), calls=%async_computation.2 | async-start | bytes 262144 | tf_op jit(solution)/shard_map/while/body/eval_jaxpr/all_to_all | solution.py:187
  700.1 12.6 %all-to-all-start.1 = ((bf16[16,1,2,2048]{3,2,1,0:T(2,128)(2,1)}), bf16[16,1,2,2048]{3,2,1,0:T(2,128)(2,1)S(1)}, u32[]{:S(2)}, u32[]{:S(2)}) async-start(bf16[16,1,2,2048]{3,2,1,0:T(2,128)(2,1)} %bitcast.444), calls=%async_computation.1 | async-start | bytes 262144 | tf_op jit(solution)/shard_map/while/body/eval_jaxpr/all_to_all | solution.py:182
  717.8 12.0 %all-to-all-start.2 = ((bf16[16,1,2,2048]{3,2,1,0:T(2,128)(2,1)}), bf16[16,1,2,2048]{3,2,1,0:T(2,128)(2,1)S(1)}, u32[]{:S(2)}, u32[]{:S(2)}) async-start(bf16[16,1,2,2048]{3,2,1,0:T(2,128)(2,1)} %copy.84), calls=%async_computation.2 | async-start | bytes 262144 | tf_op jit(solution)/shard_map/while/body/eval_jaxpr/all_to_all | solution.py:187
  745.0 12.6 %all-to-all-start.1 = ((bf16[16,1,2,2048]{3,2,1,0:T(2,128)(2,1)}), bf16[16,1,2,2048]{3,2,1,0:T(2,128)(2,1)S(1)}, u32[]{:S(2)}, u32[]{:S(2)}) async-start(bf16[16,1,2,2048]{3,2,1,0:T(2,128)(2,1)} %bitcast.444), calls=%async_computation.1 | async-start | bytes 262144 | tf_op jit(solution)/shard_map/while/body/eval_jaxpr/all_to_all | solution.py:182
  762.7 12.0 %all-to-all-start.2 = ((bf16[16,1,2,2048]{3,2,1,0:T(2,128)(2,1)}), bf16[16,1,2,2048]{3,2,1,0:T(2,128)(2,1)S(1)}, u32[]{:S(2)}, u32[]{:S(2)}) async-start(bf16[16,1,2,2048]{3,2,1,0:T(2,128)(2,1)} %copy.84), calls=%async_computation.2 | async-start | bytes 262144 | tf_op jit(solution)/shard_map/while/body/eval_jaxpr/all_to_all | solution.py:187
  789.9 12.6 %all-to-all-start.1 = ((bf16[16,1,2,2048]{3,2,1,0:T(2,128)(2,1)}), bf16[16,1,2,2048]{3,2,1,0:T(2,128)(2,1)S(1)}, u32[]{:S(2)}, u32[]{:S(2)}) async-start(bf16[16,1,2,2048]{3,2,1,0:T(2,128)(2,1)} %bitcast.444), calls=%async_computation.1 | async-start | bytes 262144 | tf_op jit(solution)/shard_map/while/body/eval_jaxpr/all_to_all | solution.py:182
  807.6 12.0 %all-to-all-start.2 = ((bf16[16,1,2,2048]{3,2,1,0:T(2,128)(2,1)}), bf16[16,1,2,2048]{3,2,1,0:T(2,128)(2,1)S(1)}, u32[]{:S(2)}, u32[]{:S(2)}) async-start(bf16[16,1,2,2048]{3,2,1,0:T(2,128)(2,1)} %copy.84), calls=%async_computation.2 | async-start | bytes 262144 | tf_op jit(solution)/shard_map/while/body/eval_jaxpr/all_to_all | solution.py:187
  834.8 12.6 %all-to-all-start.1 = ((bf16[16,1,2,2048]{3,2,1,0:T(2,128)(2,1)}), bf16[16,1,2,2048]{3,2,1,0:T(2,128)(2,1)S(1)}, u32[]{:S(2)}, u32[]{:S(2)}) async-start(bf16[16,1,2,2048]{3,2,1,0:T(2,128)(2,1)} %bitcast.444), calls=%async_computation.1 | async-start | bytes 262144 | tf_op jit(solution)/shard_map/while/body/eval_jaxpr/all_to_all | solution.py:182
  852.5 12.0 %all-to-all-start.2 = ((bf16[16,1,2,2048]{3,2,1,0:T(2,128)(2,1)}), bf16[16,1,2,2048]{3,2,1,0:T(2,128)(2,1)S(1)}, u32[]{:S(2)}, u32[]{:S(2)}) async-start(bf16[16,1,2,2048]{3,2,1,0:T(2,128)(2,1)} %copy.84), calls=%async_computation.2 | async-start | bytes 262144 | tf_op jit(solution)/shard_map/while/body/eval_jaxpr/all_to_all | solution.py:187
  879.7 12.6 %all-to-all-start.1 = ((bf16[16,1,2,2048]{3,2,1,0:T(2,128)(2,1)}), bf16[16,1,2,2048]{3,2,1,0:T(2,128)(2,1)S(1)}, u32[]{:S(2)}, u32[]{:S(2)}) async-start(bf16[16,1,2,2048]{3,2,1,0:T(2,128)(2,1)} %bitcast.444), calls=%async_computation.1 | async-start | bytes 262144 | tf_op jit(solution)/shard_map/while/body/eval_jaxpr/all_to_all | solution.py:182
  897.3 12.0 %all-to-all-start.2 = ((bf16[16,1,2,2048]{3,2,1,0:T(2,128)(2,1)}), bf16[16,1,2,2048]{3,2,1,0:T(2,128)(2,1)S(1)}, u32[]{:S(2)}, u32[]{:S(2)}) async-start(bf16[16,1,2,2048]{3,2,1,0:T(2,128)(2,1)} %copy.84), calls=%async_computation.2 | async-start | bytes 262144 | tf_op jit(solution)/shard_map/while/body/eval_jaxpr/all_to_all | solution.py:187
  919.0 89.0 %reduce-scatter.2.cloned.1.call-start = ((), (), s32[]{:S(2)}) async-start(), calls=%async_computation.4 | async-start | bytes 786432 | tf_op jit(solution)/shard_map/reduce_scatter | solution.py:247
  (150 other events, 1245.2 us)
Sparse Core Ops, SparseCore 0:
  919.1 87.3 all-reduce.1
Sparse Core Ops, SparseCore 1:
  922.3 13.1 reduce-scatter.1
